TPU v7x, 64 devices: a 2x2x8 block of a 4x4x8 slice. The times are simulated.
64 devices in a mesh: dp: 4 (over x, y), dcp: 16 (over z, core).
Axes of the slice: x: 2, y: 2, z: 8, core: 2. Of those that a mesh axis runs over, the one named last changes fastest.
The devices are a block of a 4x4x8 slice.
Arguments:
- q_abs: bfloat16 [32, 2, 128, 576], P('dp', None, 'dcp'), parts along dimension 0
- kv_cache: bfloat16 [32, 32, 16, 64, 576], P('dp', None, 'dcp'), parts along dimension 0
- lengths: int32 [32], P('dp'), parts along dimension 0
Outputs:
- output: bfloat16 [32, 2, 128, 512], P('dp', None, 'dcp'), parts along dimension 0
There are 4 independent parts. A program takes and returns all parts, laid end to end along the dimension named above; each array names one.
All inputs are finite; a program needn't handle non-finite values.
Results may differ from a plain program's by a relative error of at most 0.0063045.
Values are sent between devices in bfloat16 or wider.
A program may use at most 768 MiB of HBM per device.

v0:
```python
import jax
import jax.numpy as jnp
from jax import lax
from jax.sharding import PartitionSpec as P

LATENT = 512
ROPE = 64
NOPE = 128
PAGE = 64
MASKED = -1e30


def solution(mesh):
    group_size = mesh.shape['dcp']
    score_scale = (NOPE + ROPE) ** -0.5

    def local_step(q_blk, kv_blk, len_blk):
        batch_loc, tok_count, heads_loc, q_width = q_blk.shape
        rounds = kv_blk.shape[1]
        local_keys = kv_blk.reshape(batch_loc, rounds * PAGE, q_width)
        q_all = lax.all_gather(q_blk, 'dcp', axis=2, tiled=True)
        scores = jnp.einsum('bthd,bsd->bths', q_all, local_keys, preferred_element_type=jnp.float32) * score_scale
        device = lax.axis_index('dcp')
        positions = ((jnp.arange(rounds)[:, None] * group_size + device) * PAGE + jnp.arange(PAGE)[None, :]).reshape(rounds * PAGE)
        last_pos = len_blk[:, None] - tok_count + jnp.arange(tok_count)[None, :]
        visible = positions[None, None, None, :] <= last_pos[:, :, None, None]
        scores = jnp.where(visible, scores, MASKED)
        row_max = jnp.max(scores, axis=-1)
        weights = jnp.exp(scores - row_max[..., None])
        row_sum = jnp.sum(weights, axis=-1)
        part_out = jnp.einsum('bths,bsc->bthc', weights.astype(jnp.bfloat16), local_keys[:, :, :LATENT], preferred_element_type=jnp.float32)
        part_out = (part_out / row_sum[..., None]).astype(jnp.bfloat16)
        part_lse = row_max + jnp.log(row_sum)
        recv_out = lax.all_to_all(part_out, 'dcp', 2, 2, tiled=True).reshape(batch_loc, tok_count, group_size, heads_loc, LATENT)
        recv_lse = lax.all_to_all(part_lse, 'dcp', 2, 2, tiled=True).reshape(batch_loc, tok_count, group_size, heads_loc)
        total_lse = jax.nn.logsumexp(recv_lse, axis=2, keepdims=True)
        merge_w = jnp.exp(recv_lse - total_lse)
        merged = jnp.sum(merge_w[..., None] * recv_out.astype(jnp.float32), axis=2)
        return merged.astype(jnp.bfloat16)

    return jax.shard_map(local_step, mesh=mesh, in_specs=(P('dp', None, 'dcp', None), P('dp', None, 'dcp', None, None), P('dp')), out_specs=P('dp', None, 'dcp', None), check_vma=False)
```

profile of v0, /device:TPU:21, one launch (start us, length us, event | category | flops | bytes accessed | tf_op | source)
XLA Modules:
  0.0 165.3 jit_solution(6139928384335439343)
XLA Ops:
  6.5 0.0 all-gather.2.cloned.1.call-start
  6.6 0.7 all-gather.2.cloned.1.call-update
  7.3 0.1 iota_add_fusion
  7.4 0.1 add.66
  7.5 0.7 broadcast_add_fusion
  8.1 0.1 iota_add_fusion.1
  8.2 0.1 broadcast_compare_fusion
  8.4 42.3 %all-gather.2.cloned.1.call-done = bf16[8,2,128,576]{3,2,1,0:T(8,128)(2,1)} async-done(((bf16[8,2,8,576]{3,2,1,0:T(8,128)(2,1)}), bf16[8,2,128,576]{3,2,1,0:T(8,128)(2,1)}) %all-gather.2.cloned.1.call-update) | async-done | bytes 2359312 | tf_op jit(solution)/shard_map/all_gather | solution.py:21
  50.7 18.2 %fusion.1 = (f32[8,2,128]{2,1,0:T(2,128)S(1)}, f32[8,2,128,2048]{3,2,1,0:T(8,128)}) fusion(pred[8,2,2048]{2,1,0:T(4,128)(4,1)S(1)} %broadcast_compare_fusion, bf16[8,2,128,576]{3,2,1,0:T(8,128)(2,1)} %all-gather.2.cloned.1.call-done, bf16[8,2048,576,1]{2,1,3,0:T(8,128)(2,1)} %bitcast.23), kind=kOutput, calls=%fused_computation.4 | convolution fusion | flops 4844419072 | bytes 38051840 | tf_op jit(solution)/shard_map/bthd,bsd->bths/dot_general | solution.py:22
  68.9 7.9 %fusion.3 = f32[8,2,128]{2,1,0:T(2,128)S(1)} fusion(f32[8,2,128,2048]{3,2,1,0:T(8,128)} %get-tuple-element.6, f32[8,2,128]{2,1,0:T(2,128)S(1)} %get-tuple-element.5, pred[8,2,2048]{2,1,0:T(4,128)(4,1)S(1)} %broadcast_compare_fusion), kind=kLoop, calls=%fused_computation.6 | loop fusion | flops 16775168 | bytes 16826368 | tf_op jit(solution)/shard_map/reduce_sum | solution.py:30
  76.9 0.1 copy.23
  77.0 0.8 reshape.89
  77.8 4.6 %all-to-all-start = ((f32[16,1,128]{2,1,0:T(1,128)}), f32[16,1,128]{2,1,0:T(1,128)S(1)}, u32[]{:S(2)}, u32[]{:S(2)}) async-start(f32[16,1,128]{2,1,0:T(1,128)} %reshape.89), calls=%async_computation | async-start | bytes 16384 | tf_op jit(solution)/shard_map/all_to_all | solution.py:35
  82.5 13.1 %divide_convert_fusion = bf16[8,2,128,512]{3,2,1,0:T(8,128)(2,1)S(1)} fusion(bf16[8,2048,576]{2,1,0:T(8,128)(2,1)} %bitcast.24, f32[8,2,128,2048]{3,2,1,0:T(8,128)} %get-tuple-element.6, f32[8,2,128]{2,1,0:T(2,128)S(1)} %get-tuple-element.5, pred[8,2,2048]{2,1,0:T(4,128)(4,1)S(1)} %broadcast_compare_fusion, f32[8,2,128]{2,1,0:T(2,128)S(1)} %fusion.3), kind=kOutput, calls=%fused_computation.13 | convolution fusion | flops 4313841664 | bytes 35700736 | tf_op jit(solution)/shard_map/bths,bsc->bthc/dot_general | solution.py:31
  95.5 3.5 %copy.26 = bf16[8,2,128,512]{3,1,0,2:T(2,128)(2,1)} copy(bf16[8,2,128,512]{3,2,1,0:T(8,128)(2,1)S(1)} %divide_convert_fusion) | data formatting | bytes 4194304 | tf_op jit(solution)/shard_map/convert_element_type | solution.py:32
  99.1 0.0 all-to-all-done
  99.1 7.2 %all-to-all-start.1 = ((bf16[8,2,128,512]{3,1,0,2:T(2,128)(2,1)}), bf16[8,2,128,512]{3,1,0,2:T(2,128)(2,1)S(1)}, u32[]{:S(2)}, u32[]{:S(2)}) async-start(bf16[8,2,128,512]{3,1,0,2:T(2,128)(2,1)} %copy.26), calls=%async_computation.1 | async-start | bytes 4194304 | tf_op jit(solution)/shard_map/all_to_all | solution.py:34
  106.3 0.5 broadcast.66
  106.8 0.7 reduce
  107.5 0.2 reshape.90
  107.8 0.1 copy.32
  107.9 0.1 reduce_max.19
  108.0 0.1 copy.33
  108.2 0.8 copy.25
  109.0 46.2 %all-to-all-done.1 = bf16[8,2,128,512]{3,1,0,2:T(2,128)(2,1)S(1)} async-done(((bf16[8,2,128,512]{3,1,0,2:T(2,128)(2,1)}), bf16[8,2,128,512]{3,1,0,2:T(2,128)(2,1)S(1)}, u32[]{:S(2)}, u32[]{:S(2)}) %all-to-all-start.1) | async-done | bytes 2097184 | tf_op jit(solution)/shard_map/all_to_all | solution.py:34
  155.1 2.6 %fusion.9 = bf16[8,2,8,512]{3,1,0,2:T(2,128)(2,1)S(1)} fusion(bf16[8,2,16,8,512]{4,1,0,3,2:T(2,128)(2,1)S(1)} %bitcast.19, f32[8,2,16,8]{1,0,3,2:T(8,128)S(1)} %copy.25), kind=kLoop, calls=%fused_computation.12 | loop fusion | flops 3080192 | bytes 2236416 | tf_op jit(solution)/shard_map/reduce_sum | solution.py:38
  157.7 0.7 copy.27
  (6 shorter events, 0.1 us)
Async XLA Ops:
  6.5 44.2 %all-gather.2.cloned.1.call-start = ((), (), s32[]{:S(2)}) async-start(), calls=%async_computation.2 | async-start | bytes 2785280 | tf_op jit(solution)/shard_map/all_gather | solution.py:21
  77.8 21.2 %all-to-all-start = ((f32[16,1,128]{2,1,0:T(1,128)}), f32[16,1,128]{2,1,0:T(1,128)S(1)}, u32[]{:S(2)}, u32[]{:S(2)}) async-start(f32[16,1,128]{2,1,0:T(1,128)} %reshape.89), calls=%async_computation | async-start | bytes 16384 | tf_op jit(solution)/shard_map/all_to_all | solution.py:35
  99.1 56.0 %all-to-all-start.1 = ((bf16[8,2,128,512]{3,1,0,2:T(2,128)(2,1)}), bf16[8,2,128,512]{3,1,0,2:T(2,128)(2,1)S(1)}, u32[]{:S(2)}, u32[]{:S(2)}) async-start(bf16[8,2,128,512]{3,1,0,2:T(2,128)(2,1)} %copy.26), calls=%async_computation.1 | async-start | bytes 4194304 | tf_op jit(solution)/shard_map/all_to_all | solution.py:34
Sparse Core Ops, SparseCore 0:
  8.9 41.7 all-gather.1
where the time goes:
time: 166 us; the launch traced here: 165 us
  waiting for transfers between devices  89.3 us (54%)
  matrix products  31.3 us (19%)
  between operations  13.5 us (8%)
  other arithmetic  12.3 us (7%)
  starting transfers between devices  11.9 us (7%)
  local copies, waits for them, and re-layouts  7.08 us (4%)
    all_to_all x1, waiting for transfers between devices, local_step(): lax.all_to_all(part_out, 'dcp', 2, 2, tiled=True)  46.2 us
    all_gather x1, waiting for transfers between devices, local_step(): q_all = lax.all_gather(q_blk, 'dcp', axis=2, tiled=True)  42.3 us
    dot_general x1, matrix products, local_step(): jnp.einsum('bthd,bsd->bths', q_all, local_keys, preferred_element_type=jn...  18.2 us
    dot_general x1, matrix products, local_step(): jnp.einsum('bths,bsc->bthc', weights.astype(jnp.bfloat16), local_keys[:,...  13.1 us
    reduce_sum x1, other arithmetic, local_step(): row_sum = jnp.sum(weights, axis=-1)  7.94 us
    all_to_all x1, starting transfers between devices, local_step(): lax.all_to_all(part_out, 'dcp', 2, 2, tiled=True)  7.24 us
    all_to_all x1, starting transfers between devices, local_step(): lax.all_to_all(part_lse, 'dcp', 2, 2, tiled=True)  4.6 us
    convert_element_type x1, local copies, waits for them, and re-layouts, local_step(): part_out = (part_out / row_sum[..., None]).astype(jnp.bfloat16)  3.54 us
  transfers between devices with their start and end apart: 3, of which 2 were waited for; matrix products, arithmetic and copies ran while one was open for 12% of the time, Pallas kernels for 0%

commit v1 on v0

v1 whole, which is shorter than its diff:
```python
import functools
import math

import jax
import jax.numpy as jnp
from jax import lax
from jax.experimental import pallas as pl
from jax.experimental.pallas import tpu as pltpu
from jax.sharding import PartitionSpec as P

LATENT = 512
ROPE = 64
NOPE = 128
PAGE = 64
LANES = 128
PACKED = LATENT + LANES
MESH = pl.DeviceIdType.MESH


def _lse_limbs(lse):
    hi = lse.astype(jnp.bfloat16).astype(jnp.float32)
    rest = lse - hi
    mid = rest.astype(jnp.bfloat16).astype(jnp.float32)
    low = rest - mid
    shape = lse.shape[:-1] + (LANES,)
    lane = lax.broadcasted_iota(jnp.int32, shape, len(shape) - 1)
    zero = jnp.zeros(shape, jnp.float32)
    tile = jnp.where(lane == 0, hi, jnp.where(lane == 1, mid, jnp.where(lane == 2, low, zero)))
    return tile.astype(jnp.bfloat16)


def _merge(parts):
    lses = [jnp.sum(p[:, LATENT:].astype(jnp.float32), axis=-1, keepdims=True) for p in parts]
    top = functools.reduce(jnp.maximum, lses)
    ws = [jnp.exp2(x - top) for x in lses]
    total = functools.reduce(jnp.add, ws)
    inv = 1.0 / total
    out = functools.reduce(jnp.add, [p[:, :LATENT].astype(jnp.float32) * (w * inv) for p, w in zip(parts, ws)])
    return out, top + jnp.log2(total)


def _kernel(group, toks, heads, len_ref, q_hbm, kv_hbm, o_ref, kv_buf, q_buf, p_buf, d_buf, c_buf, r_buf, s_buf, pos_ref,
            sc_ref, w_ref, kv_sem, qin_sem, ql_recv, qp_recv, q_send, qp_send, d_recv, d_send, r_recv, r_send):
    batch, keys, width = kv_buf.shape
    rows = toks * heads
    chips = group // 2
    all_rows = group * rows
    scale = (NOPE + ROPE) ** -0.5 * math.log2(math.e)
    me = lax.axis_index('dcp')
    z = lax.div(me, 2)
    core = lax.rem(me, 2)
    other = 1 - core

    def chip(off):
        return lax.rem(z + off + chips, chips)

    def dev(off):
        return chip(off) * 2 + core

    partner = z * 2 + other

    def remote(src, dst, send, recv, target):
        return pltpu.make_async_remote_copy(src_ref=src, dst_ref=dst, send_sem=send, recv_sem=recv, device_id={'dcp': target}, device_id_type=MESH)

    def sign(b):
        return 1 - 2 * lax.rem(b, 2)

    own_q = pltpu.make_async_copy(q_hbm, q_buf.at[:, core, z], qin_sem)
    own_q.start()

    def kv_copy(b):
        return pltpu.make_async_copy(kv_hbm.at[b], kv_buf.at[b], kv_sem.at[b])

    def start_kv(b, carry):
        kv_copy(b).start()
        return carry

    lax.fori_loop(0, batch, start_kv, 0)

    barrier = pltpu.get_barrier_semaphore()
    for target in (dev(-1), dev(1), partner):
        pl.semaphore_signal(barrier, inc=1, device_id={'dcp': target}, device_id_type=MESH)
    pl.semaphore_wait(barrier, 3)

    def q_desc(b, src, target, slot):
        ref = q_buf.at[b, core, src]
        return remote(ref, ref, q_send.at[b], ql_recv.at[b, slot], target)

    own_q.wait()

    def send_own(b, carry):
        q_desc(b, z, dev(1), 0).start()
        q_desc(b, z, dev(-1), 3).start()
        return carry

    lax.fori_loop(0, batch, send_own, 0)

    col = lax.broadcasted_iota(jnp.int32, (rows, keys), 1)
    tok = lax.broadcasted_iota(jnp.int32, (rows, keys), 0) // heads
    pos_ref[...] = ((col // PAGE) * group + me) * PAGE + col % PAGE - tok + toks

    def q1(b):
        q_desc(b, chip(-1), partner, 0).wait_recv()
        q_desc(b, chip(-1), dev(1), 1).start()
        q_desc(b, chip(1), partner, 3).wait_recv()
        q_desc(b, chip(1), dev(-1), 4).start()

    def q2(b):
        q_desc(b, chip(-2), partner, 1).wait_recv()
        q_desc(b, chip(-2), dev(1), 2).start()
        q_desc(b, chip(2), partner, 4).wait_recv()
        q_desc(b, chip(2), dev(-1), 5).start()

    def q3(b):
        q_desc(b, chip(-3), partner, 2).wait_recv()
        q_desc(b, chip(3), partner, 5).wait_recv()
        q_desc(b, chip(-3 * sign(b)), dev(sign(b)), 6).start()

    def qp_desc(b, side):
        ref = q_buf.at[b, side]
        return remote(ref, ref, qp_send.at[b], qp_recv.at[b], partner)

    def q4(b):
        q_desc(b, chip(4), partner, 6).wait_recv()
        qp_desc(b, core).start()

    def d_desc(b):
        return remote(p_buf.at[b, other], d_buf.at[b], d_send.at[b], d_recv.at[b], partner)

    def attend(b):
        qp_desc(b, other).wait_recv()
        kv_copy(b).wait()
        q = q_buf[b].reshape(all_rows, width)
        limit = len_ref[b]
        cap = jnp.where(pos_ref[...] <= limit, jnp.inf, -jnp.inf).astype(jnp.float32)
        block = 512
        tops = []
        for j in range(keys // block):
            ks = slice(j * block, (j + 1) * block)
            s = lax.dot_general(q, kv_buf[b, ks, :], (((1,), (1,)), ((), ())), preferred_element_type=jnp.float32)
            s = jnp.minimum(s.reshape(group, rows, block) * scale, cap[None, :, ks]).reshape(all_rows, block)
            sc_ref[:, ks] = s
            tops.append(jnp.max(s, axis=-1, keepdims=True))
        top = functools.reduce(jnp.maximum, tops)
        sums = []
        for j in range(keys // block):
            ks = slice(j * block, (j + 1) * block)
            w = jnp.exp2(sc_ref[:, ks] - top)
            sums.append(jnp.sum(w, axis=-1, keepdims=True))
            w_ref[:, ks] = w.astype(jnp.bfloat16)
        total = functools.reduce(jnp.add, sums)
        out = jnp.dot(w_ref[...], kv_buf[b, :, :LATENT], preferred_element_type=jnp.float32)
        out = (out * (1.0 / total)).astype(jnp.bfloat16)
        p_buf[b, :, :, :, :LATENT] = out.reshape(2, chips, rows, LATENT)
        p_buf[b, :, :, :, LATENT:] = _lse_limbs(top + jnp.log2(total)).reshape(2, chips, rows, LANES)
        d_desc(b).start()

    def pack(ref, part):
        out, lse = part
        ref[:, :LATENT] = out.astype(jnp.bfloat16)
        ref[:, LATENT:] = _lse_limbs(lse)

    def r_desc(b, src, slot, target):
        return remote(src, r_buf.at[b, slot], r_send.at[b], r_recv.at[b, slot], target)

    def r_wait(b, slot):
        r_desc(b, r_buf.at[b, slot], slot, partner).wait_recv()

    def o0(b):
        d_desc(b).wait_recv()
        n = chips * rows
        out, lse = _merge([p_buf[b, core].reshape(n, PACKED), d_buf[b].reshape(n, PACKED)])
        c_buf[b, :, :, :LATENT] = out.astype(jnp.bfloat16).reshape(chips, rows, LATENT)
        c_buf[b, :, :, LATENT:] = _lse_limbs(lse).reshape(chips, rows, LANES)
        r_desc(b, c_buf.at[b, chip(4)], 0, dev(sign(b))).start()
        r_desc(b, c_buf.at[b, chip(-3 * sign(b))], 4, dev(-sign(b))).start()

    def hop(b, slot, off, dst, direction):
        pack(s_buf.at[b, dst], _merge([r_buf[b, slot], c_buf[b, chip(off)]]))
        r_desc(b, s_buf.at[b, dst], slot + 1, dev(direction)).start()

    def o1(b):
        s = sign(b)
        r_wait(b, 0)
        r_wait(b, 4)
        hop(b, 0, 3 * s, 0, s)
        hop(b, 4, -2 * s, 1, -s)

    def o2(b):
        s = sign(b)
        r_wait(b, 1)
        r_wait(b, 5)
        hop(b, 1, 2 * s, 2, s)
        hop(b, 5, -s, 3, -s)

    def o3(b):
        s = sign(b)
        r_wait(b, 2)
        hop(b, 2, s, 4, s)

    def o4(b):
        r_wait(b, 3)
        r_wait(b, 6)
        out, _ = _merge([r_buf[b, 3], r_buf[b, 6], c_buf[b, z]])
        o_ref[b] = out.astype(jnp.bfloat16)

    stages = [(0, q1), (2, q2), (4, q3), (6, q4), (8, o0), (10, o1), (12, o2), (14, o3), (16, o4), (7, attend)]

    def wave(w, carry):
        for off, stage in stages:
            b = w - off

            @pl.when(jnp.logical_and(b >= 0, b < batch))
            def _(stage=stage, b=b):
                stage(b)

        return carry

    lax.fori_loop(0, batch + max(off for off, _ in stages), wave, 0)

    def drain(b, carry):
        ref = q_buf.at[b, core, pl.ds(0, 7)]
        remote(ref, ref, q_send.at[b], ql_recv.at[b, 0], partner).wait_send()
        qp_desc(b, core).wait_send()
        d_desc(b).wait_send()
        remote(r_buf.at[b], r_buf.at[b], r_send.at[b], r_recv.at[b, 0], partner).wait_send()
        return carry

    lax.fori_loop(0, batch, drain, 0)


def attention(mesh, q, kv, lengths):
    batch, toks, heads, width = q.shape
    group = mesh.shape['dcp']
    chips = group // 2
    keys = kv.shape[1] * kv.shape[2] * kv.shape[3]
    rows = toks * heads
    bf16 = jnp.bfloat16
    dma = pltpu.SemaphoreType.DMA
    out = pl.pallas_call(
        functools.partial(_kernel, group, toks, heads),
        out_shape=jax.ShapeDtypeStruct((batch, rows, LATENT), bf16),
        in_specs=[
            pl.BlockSpec(memory_space=pltpu.SMEM),
            pl.BlockSpec(memory_space=pl.ANY),
            pl.BlockSpec(memory_space=pl.ANY),
        ],
        out_specs=pl.BlockSpec(memory_space=pltpu.VMEM),
        scratch_shapes=[
            pltpu.VMEM((batch, keys, width), bf16),
            pltpu.VMEM((batch, 2, chips, rows, width), bf16),
            pltpu.VMEM((batch, 2, chips, rows, PACKED), bf16),
            pltpu.VMEM((batch, chips, rows, PACKED), bf16),
            pltpu.VMEM((batch, chips, rows, PACKED), bf16),
            pltpu.VMEM((batch, 7, rows, PACKED), bf16),
            pltpu.VMEM((batch, 5, rows, PACKED), bf16),
            pltpu.VMEM((rows, keys), jnp.int32),
            pltpu.VMEM((group * rows, keys), jnp.float32),
            pltpu.VMEM((group * rows, keys), bf16),
            dma((batch,)),
            dma,
            dma((batch, 7)),
            dma((batch,)),
            dma((batch,)),
            dma((batch,)),
            dma((batch,)),
            dma((batch,)),
            dma((batch, 7)),
            dma((batch,)),
        ],
        compiler_params=pltpu.CompilerParams(collective_id=0, has_side_effects=True, vmem_limit_bytes=60 * 1024 * 1024),
        name='mla_ring',
    )(lengths, q.reshape(batch, rows, width), kv.reshape(batch, keys, width))
    return out.reshape(batch, toks, heads, LATENT)


def solution(mesh):
    return jax.shard_map(
        functools.partial(attention, mesh),
        mesh=mesh,
        in_specs=(P('dp', None, 'dcp', None), P('dp', None, 'dcp', None, None), P('dp')),
        out_specs=P('dp', None, 'dcp', None),
        check_vma=False,
    )
```

time: 166 us -> 66.1 us (0.40)
  waiting for transfers between devices: 89.3 us -> 0 us
  Pallas kernels: 0 us -> 63.9 us
  matrix products: 31.3 us -> 0 us
  between operations: 13.5 us -> 0.01 us
  other arithmetic: 12.3 us -> 0 us
  starting transfers between devices: 11.9 us -> 0 us
  local copies, waits for them, and re-layouts: 7.08 us -> 1.57 us
    pallas_call x0 -> x1, Pallas kernels: none -> 63.9 us  [attention(): pl.pallas_call(functools.partial(_kernel, group, toks, heads), out_shape=...]
    all_to_all x2 -> x0, waiting for transfers between devices: 46.2 us -> none  [the longest x1 46.2 us: local_step(): lax.all_to_all(part_out, 'dcp', 2, 2, tiled=True)]
    all_gather x1 -> x0, waiting for transfers between devices: 42.3 us -> none  [local_step(): q_all = lax.all_gather(q_blk, 'dcp', axis=2, tiled=True)]
    dot_general x2 -> x0, matrix products: 31.3 us -> none  [the longest x1 18.2 us: local_step(): jnp.einsum('bthd,bsd->bths', q_all, local_keys, preferred_element_type=jn...]
    all_to_all x2 -> x0, starting transfers between devices: 11.8 us -> none  [the longest x1 7.24 us: local_step(): lax.all_to_all(part_out, 'dcp', 2, 2, tiled=True)]
    reduce_sum x3 -> x0, other arithmetic: 10.6 us -> none  [the longest x1 7.94 us: local_step(): row_sum = jnp.sum(weights, axis=-1)]
    convert_element_type x2 -> x0, local copies, waits for them, and re-layouts: 4.27 us -> none  [the longest x1 3.54 us: local_step(): part_out = (part_out / row_sum[..., None]).astype(jnp.bfloat16)]
  transfers between devices with their start and end apart: 3 -> 0, of which waited for: 2 -> 0; matrix products, arithmetic and copies ran while one was open for 12% -> 0% of each run, Pallas kernels for 0% -> 0%
where the time goes in v1:
time: 66.1 us; the launch traced here: 65.4 us
  Pallas kernels  63.9 us (97%)
  local copies, waits for them, and re-layouts  1.57 us (2%)
    pallas_call x1, Pallas kernels, attention(): pl.pallas_call(functools.partial(_kernel, group, toks, heads), out_shape=...  63.9 us
    unnamed x1, local copies, waits for them, and re-layouts  1.57 us

profile of v1, /device:TPU:21, one launch (start us, length us, event | category | flops | bytes accessed | tf_op | source)
XLA Modules:
  0.0 65.4 jit_solution(7995681139054896565)
XLA Ops:
  0.0 63.9 %mla_ring.1 = bf16[8,16,512]{2,1,0:T(8,128)(2,1)} custom-call(s32[8]{0:T(128)} %len_ref.1, bf16[8,16,576]{2,1,0:T(8,128)(2,1)} %bitcast.5, bf16[8,2048,576]{2,1,0:T(8,128)(2,1)} %bitcast.3), custom_call_target="tpu_custom_call" | custom-call | tf_op jit(solution)/shard_map/mla_ring/pallas_call | solution.py:240
  63.9 1.6 %copy.5 = bf16[8,2,8,512]{3,2,1,0:T(8,128)(2,1)} copy(bf16[8,2,8,512]{3,2,1,0:T(8,128)(2,1)} %bitcast.4) | data formatting | bytes 262144

commit v2 on v0

v2 whole, which is shorter than its diff:
```python
import functools
import math

import jax
import jax.numpy as jnp
from jax import lax
from jax.experimental import pallas as pl
from jax.experimental.pallas import tpu as pltpu
from jax.sharding import PartitionSpec as P

LATENT = 512
ROPE = 64
NOPE = 128
PAGE = 64
LANES = 128
PAIR = 2
OUTS = PAIR * LATENT
PACKED = OUTS + LANES
MESH = pl.DeviceIdType.MESH


def _lse_limbs(lses):
    shape = lses[0].shape[:-1] + (LANES,)
    lane = lax.broadcasted_iota(jnp.int32, shape, len(shape) - 1)
    tile = jnp.zeros(shape, jnp.float32)
    for i, lse in enumerate(lses):
        hi = lse.astype(jnp.bfloat16).astype(jnp.float32)
        rest = lse - hi
        mid = rest.astype(jnp.bfloat16).astype(jnp.float32)
        for j, limb in enumerate((hi, mid, rest - mid)):
            tile = jnp.where(lane == 3 * i + j, limb, tile)
    return tile.astype(jnp.bfloat16)


def _merge(parts):
    tails = [p[:, OUTS:].astype(jnp.float32) for p in parts]
    lane = lax.broadcasted_iota(jnp.int32, tails[0].shape, 1)
    outs, lses = [], []
    for i in range(PAIR):
        mine = jnp.logical_and(lane >= 3 * i, lane < 3 * i + 3)
        ls = [jnp.sum(jnp.where(mine, t, 0.0), axis=-1, keepdims=True) for t in tails]
        top = functools.reduce(jnp.maximum, ls)
        ws = [jnp.exp2(x - top) for x in ls]
        total = functools.reduce(jnp.add, ws)
        inv = 1.0 / total
        cols = slice(i * LATENT, (i + 1) * LATENT)
        outs.append(functools.reduce(jnp.add, [p[:, cols].astype(jnp.float32) * (w * inv) for p, w in zip(parts, ws)]))
        lses.append(top + jnp.log2(total))
    return outs, lses


def _pack(outs, lses):
    return [o.astype(jnp.bfloat16) for o in outs] + [_lse_limbs(lses)]


def _kernel(group, toks, heads, len_ref, q_hbm, kv_hbm, o_ref, kv_buf, q_buf, p_buf, d_buf, c_buf, r_buf, s_buf, pos_ref,
            sc_ref, w_ref, st_ref, kv_sem, qin_sem, ql_recv, qp_recv, q_send, qp_send, d_recv, d_send, r_recv, r_send):
    batch, keys, width = kv_buf.shape
    pairs = batch // PAIR
    rows = toks * heads
    chips = group // 2
    all_rows = group * rows
    scale = (NOPE + ROPE) ** -0.5 * math.log2(math.e)
    me = lax.axis_index('dcp')
    z = lax.div(me, 2)
    core = lax.rem(me, 2)
    other = 1 - core
    partner = z * 2 + other

    def chip(off):
        return lax.rem(z + off + chips, chips)

    def dev(off):
        return chip(off) * 2 + core

    def remote(src, dst, send, recv, target):
        return pltpu.make_async_remote_copy(src_ref=src, dst_ref=dst, send_sem=send, recv_sem=recv, device_id={'dcp': target}, device_id_type=MESH)

    def sign(p):
        return 1 - 2 * lax.rem(p, 2)

    def each(lo, hi, stage):
        def step(i, carry):
            stage(i)
            return carry

        lax.fori_loop(lo, hi, step, 0)

    barrier = pltpu.get_barrier_semaphore()
    partners = [dev(off) for off in (-2, -1, 1, 2)] + [partner]
    for target in partners:
        pl.semaphore_signal(barrier, inc=1, device_id={'dcp': target}, device_id_type=MESH)

    own_q = pltpu.make_async_copy(q_hbm, q_buf.at[:, core, z], qin_sem)
    own_q.start()

    def kv_copy(b):
        return pltpu.make_async_copy(kv_hbm.at[b], kv_buf.at[b], kv_sem.at[b])

    each(0, batch, lambda b: kv_copy(b).start())

    col = lax.broadcasted_iota(jnp.int32, (rows, keys), 1)
    tok = lax.broadcasted_iota(jnp.int32, (rows, keys), 0) // heads
    pos_ref[...] = ((col // PAGE) * group + me) * PAGE + col % PAGE - tok + toks

    own_q.wait()
    pl.semaphore_wait(barrier, len(partners))

    def q_desc(p, src, target, slot):
        ref = q_buf.at[p, core, src]
        return remote(ref, ref, q_send.at[p], ql_recv.at[p, slot], target)

    def q0(p):
        q_desc(p, z, dev(1), 0).start()
        q_desc(p, z, dev(-1), 3).start()

    def q1(p):
        q_desc(p, chip(-1), partner, 0).wait_recv()
        q_desc(p, chip(-1), dev(1), 1).start()
        q_desc(p, chip(1), partner, 3).wait_recv()
        q_desc(p, chip(1), dev(-1), 4).start()

    def q2(p):
        q_desc(p, chip(-2), partner, 1).wait_recv()
        q_desc(p, chip(-2), dev(1), 2).start()
        q_desc(p, chip(2), partner, 4).wait_recv()
        q_desc(p, chip(2), dev(-1), 5).start()

    def q3(p):
        q_desc(p, chip(-3), partner, 2).wait_recv()
        q_desc(p, chip(3), partner, 5).wait_recv()
        q_desc(p, chip(-3 * sign(p)), dev(sign(p)), 6).start()

    def qp_desc(p, side):
        ref = q_buf.at[p, side]
        return remote(ref, ref, qp_send.at[p], qp_recv.at[p], partner)

    def q4(p):
        q_desc(p, chip(4), partner, 6).wait_recv()
        qp_desc(p, core).start()

    def d_desc(p):
        return remote(p_buf.at[p, other], d_buf.at[p], d_send.at[p], d_recv.at[p], partner)

    block = 256
    spans = [slice(j, j + block) for j in range(0, keys, block)]

    def scores(p, u):
        q = q_buf[p, :, :, u].reshape(all_rows, width)
        cap = jnp.where(pos_ref[...] <= len_ref[p * PAIR + u], jnp.inf, -jnp.inf).astype(jnp.float32)

        def step(ks):
            s = lax.dot_general(q, kv_buf[p * PAIR + u, ks, :], (((1,), (1,)), ((), ())), preferred_element_type=jnp.float32)
            s = jnp.minimum(s.reshape(group, rows, block) * scale, cap[None, :, ks]).reshape(all_rows, block)
            sc_ref[u, :, ks] = s
            return jnp.max(s, axis=-1, keepdims=True)

        return step

    def weigh(u, top, ks):
        w = jnp.exp2(sc_ref[u, :, ks] - top)
        w_ref[u, :, ks] = w.astype(jnp.bfloat16)
        return jnp.sum(w, axis=-1, keepdims=True)

    def spread(x):
        return jnp.broadcast_to(x, (all_rows, LANES))

    def attend_a(p):
        qp_desc(p, other).wait_recv()
        kv_copy(p * PAIR).wait()
        kv_copy(p * PAIR + 1).wait()
        first, second = scores(p, 0), scores(p, 1)
        top0 = functools.reduce(jnp.maximum, [first(ks) for ks in spans])
        tops, sums = [], []
        for ks in spans:
            tops.append(second(ks))
            sums.append(weigh(0, top0, ks))
        st_ref[0] = spread(top0)
        st_ref[1] = spread(functools.reduce(jnp.maximum, tops))
        st_ref[2] = spread(functools.reduce(jnp.add, sums))

    def attend_b(p):
        def product(u):
            return jnp.dot(w_ref[u], kv_buf[p * PAIR + u, :, :LATENT], preferred_element_type=jnp.float32)

        def keep(u, out, total):
            out = (out * (1.0 / total)).astype(jnp.bfloat16)
            p_buf[p, :, :, :, u * LATENT:(u + 1) * LATENT] = out.reshape(2, chips, rows, LATENT)

        top1 = st_ref[1][:, :1]
        total0 = st_ref[2][:, :1]
        out0 = product(0)
        total1 = functools.reduce(jnp.add, [weigh(1, top1, ks) for ks in spans])
        keep(0, out0, total0)
        tail = _lse_limbs([st_ref[0][:, :1] + jnp.log2(total0), top1 + jnp.log2(total1)])
        p_buf[p, :, :, :, OUTS:] = tail.reshape(2, chips, rows, LANES)
        keep(1, product(1), total1)
        d_desc(p).start()

    def r_desc(p, src, slot, off):
        return remote(src, r_buf.at[p, slot], r_send.at[p], r_recv.at[p, slot], dev(off))

    def r_wait(p, slot):
        r_desc(p, r_buf.at[p, slot], slot, 1).wait_recv()

    cuts = [slice(0, LATENT), slice(LATENT, OUTS), slice(OUTS, PACKED)]

    def o0(p):
        d_desc(p).wait_recv()
        n = chips * rows
        packed = _pack(*_merge([p_buf[p, core].reshape(n, PACKED), d_buf[p].reshape(n, PACKED)]))
        for cut, x in zip(cuts, packed):
            c_buf[p, :, :, cut] = x.reshape(chips, rows, x.shape[-1])
        s = sign(p)
        r_desc(p, c_buf.at[p, chip(4)], 0, 2 * s).start()
        r_desc(p, c_buf.at[p, chip(3 * s)], 1, s).start()
        r_desc(p, c_buf.at[p, chip(-3 * s)], 2, -s).start()
        r_desc(p, c_buf.at[p, chip(1)], 3, 1).start()
        r_desc(p, c_buf.at[p, chip(-1)], 4, -1).start()

    def o1(p):
        s = sign(p)
        for slot in (0, 1, 2):
            r_wait(p, slot)
        far = _pack(*_merge([c_buf[p, chip(2 * s)], r_buf[p, 0], r_buf[p, 1]]))
        near = _pack(*_merge([c_buf[p, chip(-2 * s)], r_buf[p, 2]]))
        for i, packed in enumerate((far, near)):
            for cut, x in zip(cuts, packed):
                s_buf[p, i, :, cut] = x
        r_desc(p, s_buf.at[p, 0], 5, 2 * s).start()
        r_desc(p, s_buf.at[p, 1], 6, -2 * s).start()

    def o2(p):
        for slot in (3, 4, 5, 6):
            r_wait(p, slot)
        outs, _ = _merge([c_buf[p, z]] + [r_buf[p, slot] for slot in (3, 4, 5, 6)])
        for u in range(PAIR):
            o_ref[p, u] = outs[u].astype(jnp.bfloat16)

    for stage in (q0, q1, q2, q3):
        each(0, pairs, stage)
    q4(0)

    stages = [
        (3, o1), (-1, q4), (0, attend_a), (4, o2), (1, o0), (0, attend_b),
    ]

    def wave(w, carry):
        for off, stage in stages:
            p = w - off

            @pl.when(jnp.logical_and(p >= 0, p < pairs))
            def _(stage=stage, p=p):
                stage(p)

        return carry

    lax.fori_loop(0, pairs + max(off for off, _ in stages), wave, 0)

    def drain(p, carry):
        ref = q_buf.at[p, core, pl.ds(0, 7)]
        remote(ref, ref, q_send.at[p], ql_recv.at[p, 0], partner).wait_send()
        qp_desc(p, core).wait_send()
        d_desc(p).wait_send()
        remote(r_buf.at[p], r_buf.at[p], r_send.at[p], r_recv.at[p, 0], partner).wait_send()
        return carry

    lax.fori_loop(0, pairs, drain, 0)


def attention(mesh, q, kv, lengths):
    batch, toks, heads, width = q.shape
    group = mesh.shape['dcp']
    chips = group // 2
    keys = kv.shape[1] * kv.shape[2] * kv.shape[3]
    rows = toks * heads
    pairs = batch // PAIR
    bf16 = jnp.bfloat16
    dma = pltpu.SemaphoreType.DMA
    out = pl.pallas_call(
        functools.partial(_kernel, group, toks, heads),
        out_shape=jax.ShapeDtypeStruct((pairs, PAIR, rows, LATENT), bf16),
        in_specs=[
            pl.BlockSpec(memory_space=pltpu.SMEM),
            pl.BlockSpec(memory_space=pl.ANY),
            pl.BlockSpec(memory_space=pl.ANY),
        ],
        out_specs=pl.BlockSpec(memory_space=pltpu.VMEM),
        scratch_shapes=[
            pltpu.VMEM((batch, keys, width), bf16),
            pltpu.VMEM((pairs, 2, chips, PAIR, rows, width), bf16),
            pltpu.VMEM((pairs, 2, chips, rows, PACKED), bf16),
            pltpu.VMEM((pairs, chips, rows, PACKED), bf16),
            pltpu.VMEM((pairs, chips, rows, PACKED), bf16),
            pltpu.VMEM((pairs, 7, rows, PACKED), bf16),
            pltpu.VMEM((pairs, 2, rows, PACKED), bf16),
            pltpu.VMEM((rows, keys), jnp.int32),
            pltpu.VMEM((PAIR, group * rows, keys), jnp.float32),
            pltpu.VMEM((PAIR, group * rows, keys), bf16),
            pltpu.VMEM((3, group * rows, LANES), jnp.float32),
            dma((batch,)),
            dma,
            dma((pairs, 7)),
            dma((pairs,)),
            dma((pairs,)),
            dma((pairs,)),
            dma((pairs,)),
            dma((pairs,)),
            dma((pairs, 7)),
            dma((pairs,)),
        ],
        compiler_params=pltpu.CompilerParams(collective_id=0, has_side_effects=True, vmem_limit_bytes=60 * 1024 * 1024),
        name='mla_ring',
    )(lengths, q.reshape(pairs, PAIR, rows, width), kv.reshape(batch, keys, width))
    return out.reshape(batch, toks, heads, LATENT)


def solution(mesh):
    return jax.shard_map(
        functools.partial(attention, mesh),
        mesh=mesh,
        in_specs=(P('dp', None, 'dcp', None), P('dp', None, 'dcp', None, None), P('dp')),
        out_specs=P('dp', None, 'dcp', None),
        check_vma=False,
    )
```

time: 166 us -> 54.3 us (0.33)
  waiting for transfers between devices: 89.3 us -> 0 us
  Pallas kernels: 0 us -> 51.9 us
  matrix products: 31.3 us -> 0 us
  between operations: 13.5 us -> 0.01 us
  other arithmetic: 12.3 us -> 0 us
  starting transfers between devices: 11.9 us -> 0 us
  local copies, waits for them, and re-layouts: 7.08 us -> 1.57 us
    pallas_call x0 -> x1, Pallas kernels: none -> 51.9 us  [attention(): pl.pallas_call(functools.partial(_kernel, group, toks, heads), out_shape=...]
    all_to_all x2 -> x0, waiting for transfers between devices: 46.2 us -> none  [the longest x1 46.2 us: local_step(): lax.all_to_all(part_out, 'dcp', 2, 2, tiled=True)]
    all_gather x1 -> x0, waiting for transfers between devices: 42.3 us -> none  [local_step(): q_all = lax.all_gather(q_blk, 'dcp', axis=2, tiled=True)]
    dot_general x2 -> x0, matrix products: 31.3 us -> none  [the longest x1 18.2 us: local_step(): jnp.einsum('bthd,bsd->bths', q_all, local_keys, preferred_element_type=jn...]
    all_to_all x2 -> x0, starting transfers between devices: 11.8 us -> none  [the longest x1 7.24 us: local_step(): lax.all_to_all(part_out, 'dcp', 2, 2, tiled=True)]
    reduce_sum x3 -> x0, other arithmetic: 10.6 us -> none  [the longest x1 7.94 us: local_step(): row_sum = jnp.sum(weights, axis=-1)]
    convert_element_type x2 -> x0, local copies, waits for them, and re-layouts: 4.27 us -> none  [the longest x1 3.54 us: local_step(): part_out = (part_out / row_sum[..., None]).astype(jnp.bfloat16)]
  transfers between devices with their start and end apart: 3 -> 0, of which waited for: 2 -> 0; matrix products, arithmetic and copies ran while one was open for 12% -> 0% of each run, Pallas kernels for 0% -> 0%
where the time goes in v2:
time: 54.3 us; the launch traced here: 53.5 us
  Pallas kernels  51.9 us (96%)
  local copies, waits for them, and re-layouts  1.57 us (3%)
    pallas_call x1, Pallas kernels, attention(): pl.pallas_call(functools.partial(_kernel, group, toks, heads), out_shape=...  51.9 us
    unnamed x1, local copies, waits for them, and re-layouts  1.57 us

profile of v2, /device:TPU:21, one launch (start us, length us, event | category | flops | bytes accessed | tf_op | source)
XLA Modules:
  0.0 53.5 jit_solution(2186206270779938053)
XLA Ops:
  0.0 51.9 %mla_ring.1 = bf16[4,2,16,512]{3,2,1,0:T(8,128)(2,1)} custom-call(s32[8]{0:T(128)} %len_ref.1, bf16[4,2,16,576]{3,2,1,0:T(8,128)(2,1)} %bitcast.5, bf16[8,2048,576]{2,1,0:T(8,128)(2,1)} %bitcast.3), custom_call_target="tpu_custom_call" | custom-call | tf_op jit(solution)/shard_map/mla_ring/pallas_call | solution.py:280
  52.0 1.6 %copy.5 = bf16[8,2,8,512]{3,2,1,0:T(8,128)(2,1)} copy(bf16[8,2,8,512]{3,2,1,0:T(8,128)(2,1)} %bitcast.4) | data formatting | bytes 262144

commit v3 on v2

--- a/solution.py
+++ b/solution.py
@@ -53,7 +53,7 @@
     return [o.astype(jnp.bfloat16) for o in outs] + [_lse_limbs(lses)]
 
 
-def _kernel(group, toks, heads, len_ref, q_hbm, kv_hbm, o_ref, kv_buf, q_buf, p_buf, d_buf, c_buf, r_buf, s_buf, pos_ref,
+def _kernel(group, toks, heads, len_ref, q_hbm, kv_hbm, o_ref, kv_buf, own_ref, q_buf, p_buf, d_buf, c_buf, r_buf, s_buf, pos_ref,
             sc_ref, w_ref, st_ref, kv_sem, qin_sem, ql_recv, qp_recv, q_send, qp_send, d_recv, d_send, r_recv, r_send):
     batch, keys, width = kv_buf.shape
     pairs = batch // PAIR
@@ -91,7 +91,7 @@
     for target in partners:
         pl.semaphore_signal(barrier, inc=1, device_id={'dcp': target}, device_id_type=MESH)
 
-    own_q = pltpu.make_async_copy(q_hbm, q_buf.at[:, core, z], qin_sem)
+    own_q = pltpu.make_async_copy(q_hbm, own_ref, qin_sem)
     own_q.start()
 
     def kv_copy(b):
@@ -104,39 +104,39 @@
     pos_ref[...] = ((col // PAGE) * group + me) * PAGE + col % PAGE - tok + toks
 
     own_q.wait()
+    for p in range(pairs):
+        for u in range(PAIR):
+            q_buf[p, core, z, :, u * LATENT:(u + 1) * LATENT] = own_ref[p, u, :, :LATENT]
+        q_buf[p, core, z, :, OUTS:] = jnp.concatenate([own_ref[p, u, :, LATENT:] for u in range(PAIR)], axis=-1)
     pl.semaphore_wait(barrier, len(partners))
 
     def q_desc(p, src, target, slot):
         ref = q_buf.at[p, core, src]
         return remote(ref, ref, q_send.at[p], ql_recv.at[p, slot], target)
 
-    def q0(p):
+    def q_far(p):
+        q_desc(p, z, dev(2), 1).start()
+        q_desc(p, z, dev(-2), 4).start()
+
+    def q_near(p):
         q_desc(p, z, dev(1), 0).start()
         q_desc(p, z, dev(-1), 3).start()
 
-    def q1(p):
-        q_desc(p, chip(-1), partner, 0).wait_recv()
-        q_desc(p, chip(-1), dev(1), 1).start()
-        q_desc(p, chip(1), partner, 3).wait_recv()
-        q_desc(p, chip(1), dev(-1), 4).start()
-
-    def q2(p):
+    def q_relay(p):
         q_desc(p, chip(-2), partner, 1).wait_recv()
+        q_desc(p, chip(2), partner, 4).wait_recv()
+        s = sign(p)
+        q_desc(p, chip(-2 * s), dev(2 * s), 6).start()
         q_desc(p, chip(-2), dev(1), 2).start()
-        q_desc(p, chip(2), partner, 4).wait_recv()
         q_desc(p, chip(2), dev(-1), 5).start()
-
-    def q3(p):
-        q_desc(p, chip(-3), partner, 2).wait_recv()
-        q_desc(p, chip(3), partner, 5).wait_recv()
-        q_desc(p, chip(-3 * sign(p)), dev(sign(p)), 6).start()
 
     def qp_desc(p, side):
         ref = q_buf.at[p, side]
         return remote(ref, ref, qp_send.at[p], qp_recv.at[p], partner)
 
-    def q4(p):
-        q_desc(p, chip(4), partner, 6).wait_recv()
+    def q_last(p):
+        for off, slot in ((-1, 0), (1, 3), (-3, 2), (3, 5), (4, 6)):
+            q_desc(p, chip(off), partner, slot).wait_recv()
         qp_desc(p, core).start()
 
     def d_desc(p):
@@ -146,7 +146,10 @@
     spans = [slice(j, j + block) for j in range(0, keys, block)]
 
     def scores(p, u):
-        q = q_buf[p, :, :, u].reshape(all_rows, width)
+        q = jnp.concatenate([
+            q_buf[p, :, :, :, u * LATENT:(u + 1) * LATENT].reshape(all_rows, LATENT),
+            q_buf[p, :, :, :, OUTS + u * ROPE:OUTS + (u + 1) * ROPE].reshape(all_rows, ROPE),
+        ], axis=-1)
         cap = jnp.where(pos_ref[...] <= len_ref[p * PAIR + u], jnp.inf, -jnp.inf).astype(jnp.float32)
 
         def step(ks):
@@ -237,25 +240,37 @@
         for u in range(PAIR):
             o_ref[p, u] = outs[u].astype(jnp.bfloat16)
 
-    for stage in (q0, q1, q2, q3):
-        each(0, pairs, stage)
-    q4(0)
-
-    stages = [
-        (3, o1), (-1, q4), (0, attend_a), (4, o2), (1, o0), (0, attend_b),
+    for stage, p in ((q_far, 0), (q_near, 0), (q_far, 1), (q_relay, 0), (q_near, 1), (q_far, 2), (q_relay, 1), (q_near, 2), (q_far, 3), (q_last, 0)):
+        stage(p)
+    late_q = [
+        [(0, [(q_last, 1), (q_relay, 2), (q_near, 3)]), (1, [(q_relay, 3)]), (2, [(q_last, 3)])],
+        [(2, [(q_last, 2)])],
     ]
 
-    def wave(w, carry):
-        for off, stage in stages:
-            p = w - off
+    def run(w, todo):
+        for at, stage in todo:
+            p = w - at
 
             @pl.when(jnp.logical_and(p >= 0, p < pairs))
             def _(stage=stage, p=p):
                 stage(p)
 
+    def run_q(w, todo):
+        for at, steps in todo:
+
+            @pl.when(w == at)
+            def _(steps=steps):
+                for stage, p in steps:
+                    stage(p)
+
+    def wave(w, carry):
+        run_q(w, late_q[1])
+        run(w, [(3, o1), (4, o2), (0, attend_a)])
+        run_q(w, late_q[0])
+        run(w, [(1, o0), (0, attend_b)])
         return carry
 
-    lax.fori_loop(0, pairs + max(off for off, _ in stages), wave, 0)
+    lax.fori_loop(0, pairs + 4, wave, 0)
 
     def drain(p, carry):
         ref = q_buf.at[p, core, pl.ds(0, 7)]
@@ -288,7 +303,8 @@
         out_specs=pl.BlockSpec(memory_space=pltpu.VMEM),
         scratch_shapes=[
             pltpu.VMEM((batch, keys, width), bf16),
-            pltpu.VMEM((pairs, 2, chips, PAIR, rows, width), bf16),
+            pltpu.VMEM((pairs, PAIR, rows, width), bf16),
+            pltpu.VMEM((pairs, 2, chips, rows, PACKED), bf16),
             pltpu.VMEM((pairs, 2, chips, rows, PACKED), bf16),
             pltpu.VMEM((pairs, chips, rows, PACKED), bf16),
             pltpu.VMEM((pairs, chips, rows, PACKED), bf16),

time: 54.3 us -> 51.7 us (0.952)
  Pallas kernels: 51.9 us -> 49.8 us
    pallas_call x1, Pallas kernels: 51.9 us -> 49.8 us  [attention(): pl.pallas_call(functools.partial(_kernel, group, toks, heads), out_shape=...]
where the time goes in v3:
time: 51.7 us; the launch traced here: 51.4 us
  Pallas kernels  49.8 us (96%)
  local copies, waits for them, and re-layouts  1.57 us (3%)
    pallas_call x1, Pallas kernels, attention(): pl.pallas_call(functools.partial(_kernel, group, toks, heads), out_shape=...  49.8 us
    unnamed x1, local copies, waits for them, and re-layouts  1.57 us

profile of v3, /device:TPU:21, one launch (start us, length us, event | category | flops | bytes accessed | tf_op | source)
XLA Modules:
  0.0 51.4 jit_solution(14968961168231443364)
XLA Ops:
  0.0 49.8 %mla_ring.1 = bf16[4,2,16,512]{3,2,1,0:T(8,128)(2,1)} custom-call(s32[8]{0:T(128)} %len_ref.1, bf16[4,2,16,576]{3,2,1,0:T(8,128)(2,1)} %bitcast.5, bf16[8,2048,576]{2,1,0:T(8,128)(2,1)} %bitcast.3), custom_call_target="tpu_custom_call" | custom-call | tf_op jit(solution)/shard_map/mla_ring/pallas_call | solution.py:295
  49.8 1.6 %copy.5 = bf16[8,2,8,512]{3,2,1,0:T(8,128)(2,1)} copy(bf16[8,2,8,512]{3,2,1,0:T(8,128)(2,1)} %bitcast.4) | data formatting | bytes 262144

commit v4 on v0

v4 whole, which is shorter than its diff:
```python
import functools
import math
import types

import jax
import jax.numpy as jnp
from jax import lax
from jax.experimental import pallas as pl
from jax.experimental.pallas import tpu as pltpu
from jax.sharding import PartitionSpec as P

LATENT = 512
ROPE = 64
NOPE = 128
PAGE = 64
LANES = 128
UNITS = ((2, 3), (1, 2))
MESH = pl.DeviceIdType.MESH


def _lse_limbs(lses):
    shape = lses[0].shape[:-1] + (LANES,)
    lane = lax.broadcasted_iota(jnp.int32, shape, len(shape) - 1)
    tile = jnp.zeros(shape, jnp.float32)
    for i, lse in enumerate(lses):
        hi = lse.astype(jnp.bfloat16).astype(jnp.float32)
        rest = lse - hi
        mid = rest.astype(jnp.bfloat16).astype(jnp.float32)
        for j, limb in enumerate((hi, mid, rest - mid)):
            tile = jnp.where(lane == 3 * i + j, limb, tile)
    return tile.astype(jnp.bfloat16)


def _merge(parts):
    count = parts[0].shape[1] // LATENT
    tails = [p[:, count * LATENT:].astype(jnp.float32) for p in parts]
    lane = lax.broadcasted_iota(jnp.int32, tails[0].shape, 1)
    outs, lses = [], []
    for i in range(count):
        mine = jnp.logical_and(lane >= 3 * i, lane < 3 * i + 3)
        ls = [jnp.sum(jnp.where(mine, t, 0.0), axis=-1, keepdims=True) for t in tails]
        top = functools.reduce(jnp.maximum, ls)
        ws = [jnp.exp2(x - top) for x in ls]
        total = functools.reduce(jnp.add, ws)
        inv = 1.0 / total
        cols = slice(i * LATENT, (i + 1) * LATENT)
        outs.append(functools.reduce(jnp.add, [p[:, cols].astype(jnp.float32) * (w * inv) for p, w in zip(parts, ws)]))
        lses.append(top + jnp.log2(total))
    return outs, lses


def _pack(outs, lses):
    return [o.astype(jnp.bfloat16) for o in outs] + [_lse_limbs(lses)]


def _kernel(group, toks, heads, len_ref, q_hbm, kv_hbm, o_ref, kv_buf, own_ref, pos_ref, sc_ref, w_ref, st_ref, kv_sem, qin_sem, *sets):
    batch, keys, width = kv_buf.shape
    rows = toks * heads
    chips = group // 2
    all_rows = group * rows
    scale = (NOPE + ROPE) ** -0.5 * math.log2(math.e)
    me = lax.axis_index('dcp')
    z = lax.div(me, 2)
    core = lax.rem(me, 2)
    other = 1 - core
    partner = z * 2 + other

    def chip(off):
        return lax.rem(z + off + chips, chips)

    def dev(off):
        return chip(off) * 2 + core

    def remote(src, dst, send, recv, target):
        return pltpu.make_async_remote_copy(src_ref=src, dst_ref=dst, send_sem=send, recv_sem=recv, device_id={'dcp': target}, device_id_type=MESH)

    def sign(p):
        return 1 - 2 * lax.rem(p, 2)

    def each(lo, hi, stage):
        def step(i, carry):
            stage(i)
            return carry

        lax.fori_loop(lo, hi, step, 0)

    barrier = pltpu.get_barrier_semaphore()
    partners = [dev(off) for off in (-2, -1, 1, 2)] + [partner]
    for target in partners:
        pl.semaphore_signal(barrier, inc=1, device_id={'dcp': target}, device_id_type=MESH)

    own_q = pltpu.make_async_copy(q_hbm, own_ref, qin_sem)
    own_q.start()

    def kv_copy(b):
        return pltpu.make_async_copy(kv_hbm.at[b], kv_buf.at[b], kv_sem.at[b])

    each(0, batch, lambda b: kv_copy(b).start())

    col = lax.broadcasted_iota(jnp.int32, (rows, keys), 1)
    tok = lax.broadcasted_iota(jnp.int32, (rows, keys), 0) // heads
    pos_ref[...] = ((col // PAGE) * group + me) * PAGE + col % PAGE - tok + toks

    own_q.wait()
    block = 256
    spans = [slice(j, j + block) for j in range(0, keys, block)]

    def unit_set(count, units, first, q_buf, p_buf, d_buf, c_buf, r_buf, s_buf, ql_recv, qp_recv, q_send, qp_send, d_recv, d_send, r_recv, r_send):
        outs = count * LATENT
        packed_width = outs + LANES

        def q_pack():
            for p in range(units):
                for u in range(count):
                    q_buf[p, core, z, :, u * LATENT:(u + 1) * LATENT] = own_ref[first + p * count + u, :, :LATENT]
                ropes = [own_ref[first + p * count + u, :, LATENT:] for u in range(count)]
                q_buf[p, core, z, :, outs:outs + count * ROPE] = jnp.concatenate(ropes, axis=-1)
                if count * ROPE < LANES:
                    q_buf[p, core, z, :, outs + count * ROPE:] = jnp.zeros((rows, LANES - count * ROPE), jnp.bfloat16)

        def q_desc(p, src, target, slot):
            ref = q_buf.at[p, core, src]
            return remote(ref, ref, q_send.at[p], ql_recv.at[p, slot], target)

        def q_far(p):
            q_desc(p, z, dev(2), 1).start()
            q_desc(p, z, dev(-2), 4).start()

        def q_near(p):
            q_desc(p, z, dev(1), 0).start()
            q_desc(p, z, dev(-1), 3).start()

        def q_relay(p):
            q_desc(p, chip(-2), partner, 1).wait_recv()
            q_desc(p, chip(2), partner, 4).wait_recv()
            s = sign(p)
            q_desc(p, chip(-2 * s), dev(2 * s), 6).start()
            q_desc(p, chip(-2), dev(1), 2).start()
            q_desc(p, chip(2), dev(-1), 5).start()

        def qp_desc(p, side):
            ref = q_buf.at[p, side]
            return remote(ref, ref, qp_send.at[p], qp_recv.at[p], partner)

        def q_last(p):
            for off, slot in ((-1, 0), (1, 3), (-3, 2), (3, 5), (4, 6)):
                q_desc(p, chip(off), partner, slot).wait_recv()
            qp_desc(p, core).start()

        def d_desc(p):
            return remote(p_buf.at[p, other], d_buf.at[p], d_send.at[p], d_recv.at[p], partner)

        def scores(p, u):
            q = jnp.concatenate([
                q_buf[p, :, :, :, u * LATENT:(u + 1) * LATENT].reshape(all_rows, LATENT),
                q_buf[p, :, :, :, outs + u * ROPE:outs + (u + 1) * ROPE].reshape(all_rows, ROPE),
            ], axis=-1)
            cap = jnp.where(pos_ref[...] <= len_ref[first + p * count + u], jnp.inf, -jnp.inf).astype(jnp.float32)

            def step(ks):
                s = lax.dot_general(q, kv_buf[first + p * count + u, ks, :], (((1,), (1,)), ((), ())), preferred_element_type=jnp.float32)
                s = jnp.minimum(s.reshape(group, rows, block) * scale, cap[None, :, ks]).reshape(all_rows, block)
                sc_ref[u, :, ks] = s
                return jnp.max(s, axis=-1, keepdims=True)

            return step

        def weigh(u, top, ks):
            w = jnp.exp2(sc_ref[u, :, ks] - top)
            w_ref[u, :, ks] = w.astype(jnp.bfloat16)
            return jnp.sum(w, axis=-1, keepdims=True)

        def spread(x):
            return jnp.broadcast_to(x, (all_rows, LANES))

        def attend_a(p):
            qp_desc(p, other).wait_recv()
            for u in range(count):
                kv_copy(first + p * count + u).wait()
            steps = [scores(p, u) for u in range(count)]
            top0 = functools.reduce(jnp.maximum, [steps[0](ks) for ks in spans])
            st_ref[0] = spread(top0)
            if count == 1:
                return
            tops, sums = [], []
            for ks in spans:
                tops.append(steps[1](ks))
                sums.append(weigh(0, top0, ks))
            st_ref[1] = spread(functools.reduce(jnp.maximum, tops))
            st_ref[2] = spread(functools.reduce(jnp.add, sums))

        def attend_b(p):
            def product(u):
                return jnp.dot(w_ref[u], kv_buf[first + p * count + u, :, :LATENT], preferred_element_type=jnp.float32)

            def keep(u, out, total):
                out = (out * (1.0 / total)).astype(jnp.bfloat16)
                p_buf[p, :, :, :, u * LATENT:(u + 1) * LATENT] = out.reshape(2, chips, rows, LATENT)

            def close(tops, totals):
                tail = _lse_limbs([top + jnp.log2(total) for top, total in zip(tops, totals)])
                p_buf[p, :, :, :, outs:] = tail.reshape(2, chips, rows, LANES)

            top0 = st_ref[0][:, :1]
            if count == 1:
                total0 = functools.reduce(jnp.add, [weigh(0, top0, ks) for ks in spans])
                close([top0], [total0])
                keep(0, product(0), total0)
            else:
                top1 = st_ref[1][:, :1]
                total0 = st_ref[2][:, :1]
                out0 = product(0)
                total1 = functools.reduce(jnp.add, [weigh(1, top1, ks) for ks in spans])
                keep(0, out0, total0)
                close([top0, top1], [total0, total1])
                keep(1, product(1), total1)
            d_desc(p).start()

        def r_desc(p, src, slot, off):
            return remote(src, r_buf.at[p, slot], r_send.at[p], r_recv.at[p, slot], dev(off))

        def r_wait(p, slot):
            r_desc(p, r_buf.at[p, slot], slot, 1).wait_recv()

        cuts = [slice(u * LATENT, (u + 1) * LATENT) for u in range(count)] + [slice(outs, packed_width)]

        def o0(p):
            d_desc(p).wait_recv()
            n = chips * rows
            packed = _pack(*_merge([p_buf[p, core].reshape(n, packed_width), d_buf[p].reshape(n, packed_width)]))
            for cut, x in zip(cuts, packed):
                c_buf[p, :, :, cut] = x.reshape(chips, rows, x.shape[-1])
            s = sign(p)
            r_desc(p, c_buf.at[p, chip(4)], 0, 2 * s).start()
            r_desc(p, c_buf.at[p, chip(3 * s)], 1, s).start()
            r_desc(p, c_buf.at[p, chip(-3 * s)], 2, -s).start()
            r_desc(p, c_buf.at[p, chip(1)], 3, 1).start()
            r_desc(p, c_buf.at[p, chip(-1)], 4, -1).start()

        def o1(p):
            s = sign(p)
            for slot in (0, 1, 2):
                r_wait(p, slot)
            far = _pack(*_merge([c_buf[p, chip(2 * s)], r_buf[p, 0], r_buf[p, 1]]))
            near = _pack(*_merge([c_buf[p, chip(-2 * s)], r_buf[p, 2]]))
            for i, packed in enumerate((far, near)):
                for cut, x in zip(cuts, packed):
                    s_buf[p, i, :, cut] = x
            r_desc(p, s_buf.at[p, 0], 5, 2 * s).start()
            r_desc(p, s_buf.at[p, 1], 6, -2 * s).start()

        def o2(p):
            for slot in (3, 4, 5, 6):
                r_wait(p, slot)
            merged, _ = _merge([c_buf[p, z]] + [r_buf[p, slot] for slot in (3, 4, 5, 6)])
            for u in range(count):
                o_ref[first + p * count + u] = merged[u].astype(jnp.bfloat16)

        def drain(p):
            ref = q_buf.at[p, core, pl.ds(0, 7)]
            remote(ref, ref, q_send.at[p], ql_recv.at[p, 0], partner).wait_send()
            qp_desc(p, core).wait_send()
            d_desc(p).wait_send()
            remote(r_buf.at[p], r_buf.at[p], r_send.at[p], r_recv.at[p, 0], partner).wait_send()

        return types.SimpleNamespace(
            pack=q_pack, far=q_far, near=q_near, relay=q_relay, last=q_last, attend_a=attend_a, attend_b=attend_b,
            o0=o0, o1=o1, o2=o2, drain=drain,
        )

    size = len(sets) // len(UNITS)
    built, start = [], 0
    for i, (count, units) in enumerate(UNITS):
        built.append(unit_set(count, units, start, *sets[i * size:(i + 1) * size]))
        start += count * units
    two, one = built
    two.pack()
    one.pack()
    pl.semaphore_wait(barrier, len(partners))

    two.far(0)
    two.near(0)
    two.far(1)
    two.relay(0)
    two.near(1)
    two.far(2)
    two.relay(1)
    two.near(2)
    one.far(0)
    one.far(1)
    two.last(0)

    def when(w, lo, hi, stage, p):
        @pl.when(jnp.logical_and(w >= lo, w < hi))
        def _():
            stage(p)

    def wave(w, carry):
        two.attend_a(w)

        @pl.when(w == 0)
        def _():
            two.last(1)
            two.relay(2)
            one.near(0)
            one.near(1)

        @pl.when(w == 1)
        def _():
            two.last(2)
            one.relay(0)
            one.relay(1)

        when(w, 2, 3, one.last, 0)
        when(w, 1, 3, two.o0, w - 1)
        two.attend_b(w)
        return carry

    lax.fori_loop(0, UNITS[0][1], wave, 0)
    two.o1(0)
    one.attend_a(0)
    one.last(1)
    two.o0(2)
    one.attend_b(0)
    two.o1(1)
    one.attend_a(1)
    one.o0(0)
    one.attend_b(1)
    one.o0(1)
    two.o2(0)
    two.o1(2)
    one.o1(0)
    one.o1(1)
    two.o2(1)
    two.o2(2)
    one.o2(0)
    one.o2(1)
    each(0, UNITS[0][1], two.drain)
    each(0, UNITS[1][1], one.drain)


def attention(mesh, q, kv, lengths):
    batch, toks, heads, width = q.shape
    group = mesh.shape['dcp']
    chips = group // 2
    keys = kv.shape[1] * kv.shape[2] * kv.shape[3]
    rows = toks * heads
    bf16 = jnp.bfloat16
    dma = pltpu.SemaphoreType.DMA
    sets = []
    for count, units in UNITS:
        packed = count * LATENT + LANES
        sets += [
            pltpu.VMEM((units, 2, chips, rows, packed), bf16),
            pltpu.VMEM((units, 2, chips, rows, packed), bf16),
            pltpu.VMEM((units, chips, rows, packed), bf16),
            pltpu.VMEM((units, chips, rows, packed), bf16),
            pltpu.VMEM((units, 7, rows, packed), bf16),
            pltpu.VMEM((units, 2, rows, packed), bf16),
            dma((units, 7)),
            dma((units,)),
            dma((units,)),
            dma((units,)),
            dma((units,)),
            dma((units,)),
            dma((units, 7)),
            dma((units,)),
        ]
    out = pl.pallas_call(
        functools.partial(_kernel, group, toks, heads),
        out_shape=jax.ShapeDtypeStruct((batch, rows, LATENT), bf16),
        in_specs=[
            pl.BlockSpec(memory_space=pltpu.SMEM),
            pl.BlockSpec(memory_space=pl.ANY),
            pl.BlockSpec(memory_space=pl.ANY),
        ],
        out_specs=pl.BlockSpec(memory_space=pltpu.VMEM),
        scratch_shapes=[
            pltpu.VMEM((batch, keys, width), bf16),
            pltpu.VMEM((batch, rows, width), bf16),
            pltpu.VMEM((rows, keys), jnp.int32),
            pltpu.VMEM((2, group * rows, keys), jnp.float32),
            pltpu.VMEM((2, group * rows, keys), bf16),
            pltpu.VMEM((3, group * rows, LANES), jnp.float32),
            dma((batch,)),
            dma,
        ] + sets,
        compiler_params=pltpu.CompilerParams(collective_id=0, has_side_effects=True, vmem_limit_bytes=60 * 1024 * 1024),
        name='mla_ring',
    )(lengths, q.reshape(batch, rows, width), kv.reshape(batch, keys, width))
    return out.reshape(batch, toks, heads, LATENT)


def solution(mesh):
    return jax.shard_map(
        functools.partial(attention, mesh),
        mesh=mesh,
        in_specs=(P('dp', None, 'dcp', None), P('dp', None, 'dcp', None, None), P('dp')),
        out_specs=P('dp', None, 'dcp', None),
        check_vma=False,
    )
```

time: 166 us -> 51.3 us (0.31)
  waiting for transfers between devices: 89.3 us -> 0 us
  Pallas kernels: 0 us -> 49.6 us
  matrix products: 31.3 us -> 0 us
  between operations: 13.5 us -> 0.01 us
  other arithmetic: 12.3 us -> 0 us
  starting transfers between devices: 11.9 us -> 0 us
  local copies, waits for them, and re-layouts: 7.08 us -> 1.57 us
    pallas_call x0 -> x1, Pallas kernels: none -> 49.6 us  [attention(): pl.pallas_call(functools.partial(_kernel, group, toks, heads), out_shape=...]
    all_to_all x2 -> x0, waiting for transfers between devices: 46.2 us -> none  [the longest x1 46.2 us: local_step(): lax.all_to_all(part_out, 'dcp', 2, 2, tiled=True)]
    all_gather x1 -> x0, waiting for transfers between devices: 42.3 us -> none  [local_step(): q_all = lax.all_gather(q_blk, 'dcp', axis=2, tiled=True)]
    dot_general x2 -> x0, matrix products: 31.3 us -> none  [the longest x1 18.2 us: local_step(): jnp.einsum('bthd,bsd->bths', q_all, local_keys, preferred_element_type=jn...]
    all_to_all x2 -> x0, starting transfers between devices: 11.8 us -> none  [the longest x1 7.24 us: local_step(): lax.all_to_all(part_out, 'dcp', 2, 2, tiled=True)]
    reduce_sum x3 -> x0, other arithmetic: 10.6 us -> none  [the longest x1 7.94 us: local_step(): row_sum = jnp.sum(weights, axis=-1)]
    convert_element_type x2 -> x0, local copies, waits for them, and re-layouts: 4.27 us -> none  [the longest x1 3.54 us: local_step(): part_out = (part_out / row_sum[..., None]).astype(jnp.bfloat16)]
  transfers between devices with their start and end apart: 3 -> 0, of which waited for: 2 -> 0; matrix products, arithmetic and copies ran while one was open for 12% -> 0% of each run, Pallas kernels for 0% -> 0%
where the time goes in v4:
time: 51.3 us; the launch traced here: 51.2 us
  Pallas kernels  49.6 us (97%)
  local copies, waits for them, and re-layouts  1.57 us (3%)
    pallas_call x1, Pallas kernels, attention(): pl.pallas_call(functools.partial(_kernel, group, toks, heads), out_shape=...  49.6 us
    unnamed x1, local copies, waits for them, and re-layouts  1.57 us

profile of v4, /device:TPU:21, one launch (start us, length us, event | category | flops | bytes accessed | tf_op | source)
XLA Modules:
  0.0 51.2 jit_solution(8413205754931325619)
XLA Ops:
  0.0 49.6 %mla_ring.1 = bf16[8,16,512]{2,1,0:T(8,128)(2,1)} custom-call(s32[8]{0:T(128)} %len_ref.1, bf16[8,16,576]{2,1,0:T(8,128)(2,1)} %bitcast.5, bf16[8,2048,576]{2,1,0:T(8,128)(2,1)} %bitcast.3), custom_call_target="tpu_custom_call" | custom-call | tf_op jit(solution)/shard_map/mla_ring/pallas_call | solution.py:369
  49.6 1.6 %copy.5 = bf16[8,2,8,512]{3,2,1,0:T(8,128)(2,1)} copy(bf16[8,2,8,512]{3,2,1,0:T(8,128)(2,1)} %bitcast.4) | data formatting | bytes 262144

commit v5 on v4

--- a/solution.py
+++ b/solution.py
@@ -53,7 +53,7 @@
     return [o.astype(jnp.bfloat16) for o in outs] + [_lse_limbs(lses)]
 
 
-def _kernel(group, toks, heads, len_ref, q_hbm, kv_hbm, o_ref, kv_buf, own_ref, pos_ref, sc_ref, w_ref, st_ref, kv_sem, qin_sem, *sets):
+def _kernel(group, toks, heads, len_ref, q_hbm, kv_hbm, o_hbm, o_ref, out_sem, kv_buf, own_ref, pos_ref, sc_ref, w_ref, st_ref, kv_sem, qin_sem, *sets):
     batch, keys, width = kv_buf.shape
     rows = toks * heads
     chips = group // 2
@@ -96,6 +96,9 @@
         return pltpu.make_async_copy(kv_hbm.at[b], kv_buf.at[b], kv_sem.at[b])
 
     each(0, batch, lambda b: kv_copy(b).start())
+
+    def out_copy(b):
+        return pltpu.make_async_copy(o_ref.at[b], o_hbm.at[b], out_sem.at[b])
 
     col = lax.broadcasted_iota(jnp.int32, (rows, keys), 1)
     tok = lax.broadcasted_iota(jnp.int32, (rows, keys), 0) // heads
@@ -255,6 +258,7 @@
             merged, _ = _merge([c_buf[p, z]] + [r_buf[p, slot] for slot in (3, 4, 5, 6)])
             for u in range(count):
                 o_ref[first + p * count + u] = merged[u].astype(jnp.bfloat16)
+                out_copy(first + p * count + u).start()
 
         def drain(p):
             ref = q_buf.at[p, core, pl.ds(0, 7)]
@@ -337,6 +341,7 @@
     one.o2(1)
     each(0, UNITS[0][1], two.drain)
     each(0, UNITS[1][1], one.drain)
+    each(0, batch, lambda b: out_copy(b).wait())
 
 
 def attention(mesh, q, kv, lengths):
@@ -374,8 +379,10 @@
             pl.BlockSpec(memory_space=pl.ANY),
             pl.BlockSpec(memory_space=pl.ANY),
         ],
-        out_specs=pl.BlockSpec(memory_space=pltpu.VMEM),
+        out_specs=pl.BlockSpec(memory_space=pl.ANY),
         scratch_shapes=[
+            pltpu.VMEM((batch, rows, LATENT), bf16),
+            dma((batch,)),
             pltpu.VMEM((batch, keys, width), bf16),
             pltpu.VMEM((batch, rows, width), bf16),
             pltpu.VMEM((rows, keys), jnp.int32),

time: 51.3 us -> 51.1 us (level)
  no operation moved by 1% of the time
where the time goes in v5:
time: 51.1 us; the launch traced here: 51 us
  Pallas kernels  49.4 us (97%)
  local copies, waits for them, and re-layouts  1.57 us (3%)
    pallas_call x1, Pallas kernels, attention(): pl.pallas_call(functools.partial(_kernel, group, toks, heads), out_shape=...  49.4 us
    unnamed x1, local copies, waits for them, and re-layouts  1.57 us

profile of v5, /device:TPU:21, one launch (start us, length us, event | category | flops | bytes accessed | tf_op | source)
XLA Modules:
  0.0 51.0 jit_solution(9070118144545921363)
XLA Ops:
  0.0 49.4 %mla_ring.1 = bf16[8,16,512]{2,1,0:T(8,128)(2,1)} custom-call(s32[8]{0:T(128)} %len_ref.1, bf16[8,16,576]{2,1,0:T(8,128)(2,1)} %bitcast.5, bf16[8,2048,576]{2,1,0:T(8,128)(2,1)} %bitcast.3), custom_call_target="tpu_custom_call" | custom-call | tf_op jit(solution)/shard_map/mla_ring/pallas_call | solution.py:374
  49.5 1.6 %copy.5 = bf16[8,2,8,512]{3,2,1,0:T(8,128)(2,1)} copy(bf16[8,2,8,512]{3,2,1,0:T(8,128)(2,1)} %bitcast.4) | data formatting | bytes 262144
